TPU v7x, 32 devices: a whole 2x2x4 slice. The times are simulated.
32 devices in a mesh: grp: 4 (over z), tm: 8 (over y, x, core).
Axes of the slice: x: 2, y: 2, z: 4, core: 2. Of those that a mesh axis runs over, the one named last changes fastest.
Arguments:
- initial: float32 [8, 16384], P('grp'), parts along dimension 0, may hold values from -1 to 1
- forcing: float32 [8, 32, 16384], P('grp', 'tm'), parts along dimension 0, may hold values from -1.8 to 1.8
- fine_blocks: float32 [16, 3, 128, 128], replicated, may hold values from -0.2 to 0.9, as said below
- coarse_blocks: float32 [16, 3, 128, 128], replicated, may hold values from -0.2 to 0.9, as said below
Outputs:
- solution: float32 [8, 32, 16384], P('grp', 'tm'), parts along dimension 0
There are 4 independent parts, one for each index of `grp`. A program takes and returns all parts, laid end to end along the dimension named above; an argument that names none is the same for every part. Nothing has to cross between parts.
Inputs may be any that keep to these rules, and one draw needn't show every extreme that they name: `fine_blocks`: 16 x 3 blocks of 128 x 128. `coarse_blocks`: 16 x 3 blocks of 128 x 128.
All inputs are finite; a program needn't handle non-finite values.
Results may differ from a plain program's by a relative error of at most 0.00013.
Values sent between devices are 32-bit elements; how exact they have to be, the bound alone decides.
A program may use at most 64 MiB of HBM per device.

v0:
```python
import functools

import jax
import jax.numpy as jnp
from jax import lax
from jax.experimental import pallas as pl
from jax.experimental.pallas import tpu as pltpu
from jax.sharding import PartitionSpec as P

M = 4
DELTA = 0.05
MESH = pl.DeviceIdType.MESH


def newton(mixing, delta_t):
    solved = mixing
    for _ in range(2):
        squared = solved * solved
        solved = (mixing + (2.0 * delta_t) * solved * squared) / (
            (1.0 - delta_t) + (3.0 * delta_t) * squared
        )
    return solved


def kernel(
    n, inst, zones, reps, pieces,
    init_hbm, forc_hbm, fine_hbm, coarse_hbm, out_ref,
    init_ref, forc_ref, raw, weights, x, ubuf, carr, rbuf, pbuf, qbuf,
    load_sem, state_sem, carr_send, carr_recv, r_send, r_recv, fwd_send,
):
    me = lax.axis_index("tm")
    blk = raw.shape[-1]
    rows = inst * reps
    coarse_dt = DELTA * M
    part = zones // pieces
    odd = lax.rem(me, 2)

    def load(which, c):
        span = pl.ds(c * part, part)
        return pltpu.make_async_copy((fine_hbm, coarse_hbm)[which].at[span], raw.at[which, span], load_sem.at[which, c])

    state_loads = [
        pltpu.make_async_copy(init_hbm, init_ref, state_sem.at[0]),
        pltpu.make_async_copy(forc_hbm, forc_ref, state_sem.at[1]),
    ]
    for c in range(pieces):
        load(0, c).start()
    for copy in state_loads:
        copy.start()

    barrier = pltpu.get_barrier_semaphore()
    for step in range(1, n):
        pl.semaphore_signal(barrier, inc=1, device_id={"tm": lax.rem(me + step, n)}, device_id_type=MESH)

    def initial_at(z):
        return jnp.concatenate(
            [init_ref[pl.ds(z * inst + i, reps, stride=zones * inst), :] for i in range(inst)], axis=0
        )

    def forcing_at(slot, z):
        return jnp.concatenate(
            [forc_ref[pl.ds((i * reps * zones + z) * M + slot, reps, stride=zones * M), :] for i in range(inst)],
            axis=0,
        )

    def emit_out(slot, z, value):
        for i in range(inst):
            out_ref[pl.ds((i * reps * zones + z) * M + slot, reps, stride=zones * M), :] = value[
                i * reps : (i + 1) * reps
            ]

    row = lax.broadcasted_iota(jnp.int32, (rows, blk), 0)

    def put(dst, z, value):
        def write(slot, v):
            high = v.astype(jnp.bfloat16)
            low = (v - high.astype(jnp.float32)).astype(jnp.bfloat16)
            x[dst, slot, :rows] = high
            x[dst, slot, rows:] = low

        write(z + 1, value)
        if z == 0:
            rolled = pltpu.roll(value, rows - 1, 0)
            write(zones + 1, jnp.where(row % reps == reps - 1, 0.0, rolled))
        if z == zones - 1:
            rolled = pltpu.roll(value, 1, 0)
            write(0, jnp.where(row % reps == 0, 0.0, rolled))

    def propagate(src, which, delta_t, emit):
        for z in range(zones):
            left = jnp.concatenate([x[src, z + k] for k in range(3)], axis=1)
            acc = jnp.dot(left, weights[which, z], preferred_element_type=jnp.float32)
            mixing = (acc[:rows, :blk] + acc[:rows, blk:]) + (acc[rows:, :blk] + acc[rows:, blk:])
            emit(z, newton(mixing, delta_t))

    def prepare(which):
        @pl.loop(0, pieces)
        def _(c):
            load(which, c).wait()
            if which == 0:

                @pl.when(c == pieces - 1)
                def _():
                    for later in range(pieces):
                        load(1, later).start()

            for zz in range(part):
                z = c * part + zz
                for k in range(3):
                    turned = raw[which, z, k].T
                    high = turned.astype(jnp.bfloat16)
                    weights[which, z, k * blk : (k + 1) * blk, :blk] = high
                    weights[which, z, k * blk : (k + 1) * blk, blk:] = (
                        turned - high.astype(jnp.float32)
                    ).astype(jnp.bfloat16)

    def fine_step(t, src, sink, keep=True):
        def emit(z, s):
            value = s + forcing_at(t, z)
            if keep:
                put(1 - src, z, value)
            sink(z, value)

        propagate(src, 0, DELTA, emit)

    def store_to(buf):
        def emit(z, value):
            buf[z] = value

        return emit

    def drop(z, value):
        pass

    prepare(0)
    for copy in state_loads:
        copy.wait()

    @pl.when(me == 0)
    def _():
        for z in range(zones):
            put(0, z, initial_at(z))
        fine_step(0, 0, drop)

    @pl.when(me > 0)
    def _():
        for z in range(zones):
            put(1, z, forcing_at(0, z))

    for t in range(1, M):
        fine_step(t, t % 2, store_to(ubuf) if t == M - 1 else drop, keep=t < M - 1)
    pl.semaphore_wait(barrier, n - 1)

    onward = pltpu.make_async_remote_copy(
        src_ref=ubuf, dst_ref=carr, send_sem=carr_send, recv_sem=carr_recv,
        device_id={"tm": lax.rem(me + 1, n)}, device_id_type=MESH,
    )

    @pl.when(me < n - 1)
    def _():
        onward.start()

    prepare(1)
    for z in range(zones):
        put(0, z, initial_at(z))
    propagate(0, 1, coarse_dt, store_to(pbuf))

    @pl.when(me == 0)
    def _():
        for z in range(zones):
            rbuf[0, z] = ubuf[z] - pbuf[z]

    @pl.when(me > 0)
    def _():
        onward.wait_recv()
        for z in range(zones):
            put(0, z, carr[z])
        propagate(0, 1, coarse_dt, store_to(qbuf))
        for t in range(M - 1):
            fine_step(t, t % 2, drop)

        def right_side(z, value):
            rbuf[me, z] = value - qbuf[z]

        fine_step(M - 1, (M - 1) % 2, right_side, keep=False)

    def share(target):
        return pltpu.make_async_remote_copy(
            src_ref=rbuf.at[me], dst_ref=rbuf.at[me], send_sem=r_send.at[target], recv_sem=r_recv.at[me],
            device_id={"tm": target}, device_id_type=MESH,
        )

    def forward(j):
        return pltpu.make_async_remote_copy(
            src_ref=rbuf.at[j], dst_ref=rbuf.at[j], send_sem=fwd_send.at[j], recv_sem=r_recv.at[j],
            device_id={"tm": lax.rem(me + n - 1, n)}, device_id_type=MESH,
        )

    for target in range(n - 1, 0, -2):

        @pl.when(me < target)
        def _():
            share(target).start()

    def chain(j, _):
        forward(j).wait_recv()

        @pl.when(jnp.logical_and(odd == 1, j < me - 1))
        def _():
            forward(j).start()

        for z in range(zones):
            put(0, z, pbuf[z] + rbuf[j, z])
        propagate(0, 1, coarse_dt, store_to(pbuf))
        return 0

    lax.fori_loop(0, me, chain, 0)
    for z in range(zones):
        emit_out(M - 1, z, pbuf[z] + rbuf[me, z])
    for t in range(M - 1):
        fine_step(t, t % 2, functools.partial(emit_out, t), keep=t < M - 2)

    @pl.when(me < n - 1)
    def _():
        onward.wait_send()

    for target in range(n - 1, 0, -2):

        @pl.when(me < target)
        def _():
            share(target).wait_send()

    def drain(j, _):
        forward(j).wait_send()
        return 0

    lax.fori_loop(0, jnp.where(odd == 1, me - 1, 0), drain, 0)


def solution(mesh):
    n = mesh.shape["tm"]

    def body(initial, forcing, fine_blocks, coarse_blocks):
        inst, slots, cells = forcing.shape
        zones, _, blk, _ = fine_blocks.shape
        blocks = cells // blk
        reps = blocks // zones
        rows = inst * reps
        assert slots == M and n % 2 == 0
        pieces = 4 if zones % 4 == 0 else 1
        init_rows = initial.reshape(inst, blocks, blk).transpose(1, 0, 2).reshape(-1, blk)
        forc_rows = forcing.reshape(inst, slots, blocks, blk).transpose(0, 2, 1, 3).reshape(-1, blk)
        state = pltpu.VMEM((zones, rows, blk), jnp.float32)
        out = pl.pallas_call(
            functools.partial(kernel, n, inst, zones, reps, pieces),
            out_shape=pltpu.VMEM(forc_rows.shape, jnp.float32),
            in_specs=[pl.BlockSpec(memory_space=pltpu.HBM)] * 4,
            out_specs=pl.BlockSpec(memory_space=pltpu.VMEM),
            scratch_shapes=[
                pltpu.VMEM(init_rows.shape, jnp.float32),
                pltpu.VMEM(forc_rows.shape, jnp.float32),
                pltpu.VMEM((2,) + fine_blocks.shape, jnp.float32),
                pltpu.VMEM((2, zones, 3 * blk, 2 * blk), jnp.bfloat16),
                pltpu.VMEM((2, zones + 2, 2 * rows, blk), jnp.bfloat16),
                state,
                state,
                pltpu.VMEM((n, zones, rows, blk), jnp.float32),
                state,
                state,
                pltpu.SemaphoreType.DMA((2, pieces)),
                pltpu.SemaphoreType.DMA((2,)),
                pltpu.SemaphoreType.DMA,
                pltpu.SemaphoreType.DMA,
                pltpu.SemaphoreType.DMA((n,)),
                pltpu.SemaphoreType.DMA((n,)),
                pltpu.SemaphoreType.DMA((n,)),
            ],
            compiler_params=pltpu.CompilerParams(collective_id=0, has_side_effects=True),
        )(init_rows, forc_rows, fine_blocks, coarse_blocks)
        return out.reshape(inst, blocks, slots, blk).transpose(0, 2, 1, 3).reshape(forcing.shape)

    in_specs = (P("grp", None), P("grp", "tm", None), P(), P())
    out_specs = P("grp", "tm", None)
    return jax.shard_map(body, mesh=mesh, in_specs=in_specs, out_specs=out_specs, check_vma=False)
```

profile of v0, /device:TPU:30, one launch (start us, length us, event | category | flops | bytes accessed | tf_op | source)
XLA Modules:
  0.0 20.2 jit_solution(137363473520324477)
XLA Ops:
  0.0 19.4 %shard_map.46 = f32[1024,128]{1,0:T(8,128)S(1)} custom-call(f32[256,128]{1,0:T(8,128)} %bitcast.17, f32[1024,128]{1,0:T(8,128)} %bitcast.16, f32[16,3,128,128]{3,2,1,0:T(8,128)} %fine_hbm.1, f32[16,3,128,128]{3,2,1,0:T(8,128)} %coarse_hbm.1), custom_call_target="tpu_custom_call" | custom-call | tf_op jit(solution)/shard_map/pallas_call | solution.py:254
  19.4 0.8 %copy.9 = f32[2,4,16384]{2,1,0:T(4,128)} copy(f32[2,4,16384]{2,1,0:T(4,128)S(1)} %bitcast.15) | data formatting | bytes 1048576
where the time goes:
time: 20.4 us; the launch traced here: 20.2 us
  Pallas kernels  19.4 us (95%)
  local copies, waits for them, and re-layouts  0.8 us (4%)
    pallas_call x1, Pallas kernels, body(): pl.pallas_call(functools.partial(kernel, n, inst, zones, reps, pieces), o...  19.4 us
    unnamed x1, local copies, waits for them, and re-layouts  0.8 us

commit v1 on v0

--- a/solution.py
+++ b/solution.py
@@ -10,6 +10,7 @@
 M = 4
 DELTA = 0.05
 MESH = pl.DeviceIdType.MESH
+F8 = jnp.float8_e4m3fn
 
 
 def newton(mixing, delta_t):
@@ -22,10 +23,13 @@
     return solved
 
 
+LIFT = 65536.0
+
+
 def kernel(
     n, inst, zones, reps, pieces,
     init_hbm, forc_hbm, fine_hbm, coarse_hbm, out_ref,
-    init_ref, forc_ref, raw, weights, x, ubuf, carr, rbuf, pbuf, qbuf,
+    init_ref, forc_ref, raw, wide, fix, x, ubuf, carr, rbuf, pbuf,
     load_sem, state_sem, carr_send, carr_recv, r_send, r_recv, fwd_send,
 ):
     me = lax.axis_index("tm")
@@ -33,6 +37,7 @@
     rows = inst * reps
     coarse_dt = DELTA * M
     part = zones // pieces
+    pairs = zones // 2
     odd = lax.rem(me, 2)
 
     def load(which, c):
@@ -86,12 +91,30 @@
             rolled = pltpu.roll(value, 1, 0)
             write(0, jnp.where(row % reps == 0, 0.0, rolled))
 
-    def propagate(src, which, delta_t, emit):
-        for z in range(zones):
-            left = jnp.concatenate([x[src, z + k] for k in range(3)], axis=1)
-            acc = jnp.dot(left, weights[which, z], preferred_element_type=jnp.float32)
-            mixing = (acc[:rows, :blk] + acc[:rows, blk:]) + (acc[rows:, :blk] + acc[rows:, blk:])
-            emit(z, newton(mixing, delta_t))
+    def propagate(src, which, delta_t, emit, turn=0):
+        for q in range(pairs):
+            p = (q + turn) % pairs
+            z = 2 * p
+
+            def left(i, stop):
+                return jnp.concatenate([x[src, z + i + k, :stop] for k in range(3)], axis=1)
+
+            main = jnp.dot(
+                jnp.concatenate([left(0, 2 * rows), left(1, 2 * rows)], axis=0),
+                wide[which, p], preferred_element_type=jnp.float32,
+            )
+            rest = jnp.dot(
+                jnp.concatenate([left(0, rows), left(1, rows)], axis=0),
+                fix[which, p], preferred_element_type=jnp.float32,
+            )
+            for i in range(2):
+                cols = slice(i * blk, (i + 1) * blk)
+                total = (
+                    main[2 * i * rows : (2 * i + 1) * rows, cols]
+                    + rest[i * rows : (i + 1) * rows, cols]
+                    + main[(2 * i + 1) * rows : (2 * i + 2) * rows, cols]
+                )
+                emit(z + i, newton(total * (1.0 / LIFT), delta_t))
 
     def prepare(which):
         @pl.loop(0, pieces)
@@ -106,22 +129,22 @@
 
             for zz in range(part):
                 z = c * part + zz
+                p = c * (part // 2) + zz // 2
+                cols = slice((zz % 2) * blk, (zz % 2 + 1) * blk)
                 for k in range(3):
-                    turned = raw[which, z, k].T
+                    turned = raw[which, z, k].T * LIFT
                     high = turned.astype(jnp.bfloat16)
-                    weights[which, z, k * blk : (k + 1) * blk, :blk] = high
-                    weights[which, z, k * blk : (k + 1) * blk, blk:] = (
-                        turned - high.astype(jnp.float32)
-                    ).astype(jnp.bfloat16)
-
-    def fine_step(t, src, sink, keep=True):
+                    wide[which, p, k * blk : (k + 1) * blk, cols] = high
+                    fix[which, p, k * blk : (k + 1) * blk, cols] = (turned - high.astype(jnp.float32)).astype(F8)
+
+    def fine_step(t, src, sink, keep=True, turn=0):
         def emit(z, s):
             value = s + forcing_at(t, z)
             if keep:
                 put(1 - src, z, value)
             sink(z, value)
 
-        propagate(src, 0, DELTA, emit)
+        propagate(src, 0, DELTA, emit, turn)
 
     def store_to(buf):
         def emit(z, value):
@@ -148,7 +171,7 @@
             put(1, z, forcing_at(0, z))
 
     for t in range(1, M):
-        fine_step(t, t % 2, store_to(ubuf) if t == M - 1 else drop, keep=t < M - 1)
+        fine_step(t, t % 2, store_to(ubuf) if t == M - 1 else drop, keep=t < M - 1, turn=t)
     pl.semaphore_wait(barrier, n - 1)
 
     onward = pltpu.make_async_remote_copy(
@@ -161,28 +184,38 @@
         onward.start()
 
     prepare(1)
-    for z in range(zones):
-        put(0, z, initial_at(z))
-    propagate(0, 1, coarse_dt, store_to(pbuf))
 
     @pl.when(me == 0)
     def _():
         for z in range(zones):
-            rbuf[0, z] = ubuf[z] - pbuf[z]
+            rbuf[0, z] = ubuf[z]
+            pbuf[z] = initial_at(z)
 
     @pl.when(me > 0)
     def _():
         onward.wait_recv()
+
+    @pl.when(me == 1)
+    def _():
         for z in range(zones):
             put(0, z, carr[z])
-        propagate(0, 1, coarse_dt, store_to(qbuf))
+            pbuf[z] = jnp.zeros((rows, blk), jnp.float32)
+
+    @pl.when(me > 1)
+    def _():
+        for z in range(zones):
+            put(0, z, carr[z])
+        propagate(0, 1, coarse_dt, store_to(pbuf))
+
+    @pl.when(me > 0)
+    def _():
         for t in range(M - 1):
-            fine_step(t, t % 2, drop)
+            fine_step(t, t % 2, drop, turn=t)
 
         def right_side(z, value):
-            rbuf[me, z] = value - qbuf[z]
-
-        fine_step(M - 1, (M - 1) % 2, right_side, keep=False)
+            rbuf[me, z] = value - pbuf[z]
+
+        fine_step(M - 1, (M - 1) % 2, right_side, keep=False, turn=M - 1)
 
     def share(target):
         return pltpu.make_async_remote_copy(
@@ -196,37 +229,61 @@
             device_id={"tm": lax.rem(me + n - 1, n)}, device_id_type=MESH,
         )
 
-    for target in range(n - 1, 0, -2):
-
-        @pl.when(me < target)
+    def sends(target):
+        return jnp.logical_and(me > 0, me < target)
+
+    for target in range(n - 1, 1, -2):
+
+        @pl.when(sends(target))
         def _():
             share(target).start()
 
-    def chain(j, _):
+    def arrive(j):
         forward(j).wait_recv()
 
         @pl.when(jnp.logical_and(odd == 1, j < me - 1))
         def _():
             forward(j).start()
 
+    @pl.when(me == 0)
+    def _():
+        for z in range(zones):
+            put(0, z, pbuf[z])
+
+    @pl.when(me == 1)
+    def _():
+        for z in range(zones):
+            put(0, z, carr[z])
+
+    @pl.when(me > 1)
+    def _():
+        arrive(1)
+        for z in range(zones):
+            put(0, z, rbuf[1, z])
+
+    def chain(j, _):
+        propagate(0, 1, coarse_dt, store_to(pbuf))
+        arrive(j)
         for z in range(zones):
             put(0, z, pbuf[z] + rbuf[j, z])
-        propagate(0, 1, coarse_dt, store_to(pbuf))
         return 0
 
-    lax.fori_loop(0, me, chain, 0)
-    for z in range(zones):
-        emit_out(M - 1, z, pbuf[z] + rbuf[me, z])
+    lax.fori_loop(2, me, chain, 0)
+
+    def corner(z, value):
+        emit_out(M - 1, z, jnp.where(me > 1, value, 0.0) + rbuf[me, z])
+
+    propagate(0, 1, coarse_dt, corner)
     for t in range(M - 1):
-        fine_step(t, t % 2, functools.partial(emit_out, t), keep=t < M - 2)
+        fine_step(t, t % 2, functools.partial(emit_out, t), keep=t < M - 2, turn=t)
 
     @pl.when(me < n - 1)
     def _():
         onward.wait_send()
 
-    for target in range(n - 1, 0, -2):
-
-        @pl.when(me < target)
+    for target in range(n - 1, 1, -2):
+
+        @pl.when(sends(target))
         def _():
             share(target).wait_send()
 
@@ -234,7 +291,7 @@
         forward(j).wait_send()
         return 0
 
-    lax.fori_loop(0, jnp.where(odd == 1, me - 1, 0), drain, 0)
+    lax.fori_loop(1, jnp.where(odd == 1, me - 1, 1), drain, 0)
 
 
 def solution(mesh):
@@ -246,7 +303,7 @@
         blocks = cells // blk
         reps = blocks // zones
         rows = inst * reps
-        assert slots == M and n % 2 == 0
+        assert slots == M and n % 2 == 0 and zones % 2 == 0
         pieces = 4 if zones % 4 == 0 else 1
         init_rows = initial.reshape(inst, blocks, blk).transpose(1, 0, 2).reshape(-1, blk)
         forc_rows = forcing.reshape(inst, slots, blocks, blk).transpose(0, 2, 1, 3).reshape(-1, blk)
@@ -260,12 +317,12 @@
                 pltpu.VMEM(init_rows.shape, jnp.float32),
                 pltpu.VMEM(forc_rows.shape, jnp.float32),
                 pltpu.VMEM((2,) + fine_blocks.shape, jnp.float32),
-                pltpu.VMEM((2, zones, 3 * blk, 2 * blk), jnp.bfloat16),
+                pltpu.VMEM((2, zones // 2, 3 * blk, 2 * blk), jnp.bfloat16),
+                pltpu.VMEM((2, zones // 2, 3 * blk, 2 * blk), F8),
                 pltpu.VMEM((2, zones + 2, 2 * rows, blk), jnp.bfloat16),
                 state,
                 state,
                 pltpu.VMEM((n, zones, rows, blk), jnp.float32),
-                state,
                 state,
                 pltpu.SemaphoreType.DMA((2, pieces)),
                 pltpu.SemaphoreType.DMA((2,)),

time: 20.4 us -> 18.8 us (0.922)
  Pallas kernels: 19.4 us -> 17.8 us
    pallas_call x1, Pallas kernels: 19.4 us -> 17.8 us  [body(): pl.pallas_call(functools.partial(kernel, n, inst, zones, reps, pieces), o...]
where the time goes in v1:
time: 18.8 us; the launch traced here: 18.6 us
  Pallas kernels  17.8 us (95%)
  local copies, waits for them, and re-layouts  0.8 us (4%)
    pallas_call x1, Pallas kernels, body(): pl.pallas_call(functools.partial(kernel, n, inst, zones, reps, pieces), o...  17.8 us
    unnamed x1, local copies, waits for them, and re-layouts  0.8 us

profile of v1, /device:TPU:30, one launch (start us, length us, event | category | flops | bytes accessed | tf_op | source)
XLA Modules:
  0.0 18.6 jit_solution(14587662634085569565)
XLA Ops:
  0.0 17.8 %shard_map.46 = f32[1024,128]{1,0:T(8,128)S(1)} custom-call(f32[256,128]{1,0:T(8,128)} %bitcast.17, f32[1024,128]{1,0:T(8,128)} %bitcast.16, f32[16,3,128,128]{3,2,1,0:T(8,128)} %fine_hbm.1, f32[16,3,128,128]{3,2,1,0:T(8,128)} %coarse_hbm.1), custom_call_target="tpu_custom_call" | custom-call | tf_op jit(solution)/shard_map/pallas_call | solution.py:311
  17.8 0.8 %copy.9 = f32[2,4,16384]{2,1,0:T(4,128)} copy(f32[2,4,16384]{2,1,0:T(4,128)S(1)} %bitcast.15) | data formatting | bytes 1048576

commit v2 on v1

v2 whole, which is shorter than its diff:
```python
import functools

import jax
import jax.numpy as jnp
from jax import lax
from jax.experimental import pallas as pl
from jax.experimental.pallas import tpu as pltpu
from jax.sharding import PartitionSpec as P

M = 4
DELTA = 0.05
MESH = pl.DeviceIdType.MESH
F8 = jnp.float8_e4m3fn


def newton(mixing, delta_t):
    solved = mixing
    for _ in range(2):
        squared = solved * solved
        solved = (mixing + (2.0 * delta_t) * solved * squared) / (
            (1.0 - delta_t) + (3.0 * delta_t) * squared
        )
    return solved


LIFTS = (2.0**8, 1.0, 2.0**10)


def kernel(
    n, inst, zones, reps, pieces,
    init_hbm, forc_hbm, fine_hbm, coarse_hbm, out_ref,
    init_ref, forc_ref, next_ref, raw, upper, lower, x, ubuf, carr, rbuf, pbuf,
    load_sem, state_sem, next_send, next_recv, carr_send, carr_recv, r_send, r_recv, fwd_send,
):
    me = lax.axis_index("tm")
    blk = raw.shape[-1]
    rows = inst * reps
    coarse_dt = DELTA * M
    part = zones // pieces
    pairs = zones // 2
    odd = lax.rem(me, 2)

    def load(which, c):
        span = pl.ds(c * part, part)
        return pltpu.make_async_copy((fine_hbm, coarse_hbm)[which].at[span], raw.at[which, span], load_sem.at[which, c])

    state_loads = [
        pltpu.make_async_copy(init_hbm, init_ref, state_sem.at[0]),
        pltpu.make_async_copy(forc_hbm, forc_ref, state_sem.at[1]),
    ]
    load(0, 0).start()
    for copy in state_loads:
        copy.start()
    for c in range(1, pieces):
        load(0, c).start()

    barrier = pltpu.get_barrier_semaphore()
    for step in range(1, n):
        pl.semaphore_signal(barrier, inc=1, device_id={"tm": lax.rem(me + step, n)}, device_id_type=MESH)

    def initial_at(z):
        return jnp.concatenate(
            [init_ref[pl.ds(z * inst + i, reps, stride=zones * inst), :] for i in range(inst)], axis=0
        )

    def forcing_at(ref, slot, z):
        return jnp.concatenate(
            [ref[pl.ds((i * reps * zones + z) * M + slot, reps, stride=zones * M), :] for i in range(inst)],
            axis=0,
        )

    def emit_out(slot, z, value):
        for i in range(inst):
            out_ref[pl.ds((i * reps * zones + z) * M + slot, reps, stride=zones * M), :] = value[
                i * reps : (i + 1) * reps
            ]

    row = lax.broadcasted_iota(jnp.int32, (rows, blk), 0)

    def put(dst, z, value):
        def write(slot, v):
            high = v.astype(jnp.bfloat16)
            low = (v - high.astype(jnp.float32)).astype(jnp.bfloat16)
            x[dst, slot, :rows] = high
            x[dst, slot, rows:] = low

        write(z + 1, value)
        if z == 0:
            rolled = pltpu.roll(value, rows - 1, 0)
            write(zones + 1, jnp.where(row % reps == reps - 1, 0.0, rolled))
        if z == zones - 1:
            rolled = pltpu.roll(value, 1, 0)
            write(0, jnp.where(row % reps == 0, 0.0, rolled))

    def propagate(src, which, delta_t, emit, turn=0, span=None):
        for q in span or range(pairs):
            p = (q + turn) % pairs
            z = 2 * p

            def left(i, stop):
                return jnp.concatenate([x[src, z + i + k, :stop] for k in range(3)], axis=1)

            tail = jnp.dot(
                jnp.concatenate([left(0, rows), left(1, rows)], axis=0),
                lower[which, p], preferred_element_type=jnp.float32,
            )
            for i in range(2):
                acc = jnp.dot(left(i, 2 * rows), upper[which, z + i], preferred_element_type=jnp.float32)
                cols = slice(i * blk, (i + 1) * blk)
                second = acc[:rows, blk:] + acc[rows:, blk:] + tail[i * rows : (i + 1) * rows, cols] * (1.0 / LIFTS[2])
                total = acc[:rows, :blk] + acc[rows:, :blk] + second
                emit(z + i, newton(total * (1.0 / LIFTS[0]), delta_t))

    def slices(which, z, p, cols):
        for k in range(3):
            span = slice(k * blk, (k + 1) * blk)
            rest = raw[which, z, k].T
            for s, lift in enumerate(LIFTS):
                if lift != 1.0:
                    rest = rest * lift
                piece = rest.astype(F8)
                if s < 2:
                    upper[which, z, span, s * blk : (s + 1) * blk] = piece
                    rest = rest - piece.astype(jnp.float32)
                else:
                    lower[which, p, span, cols] = piece

    def columns(zz):
        return slice((zz % 2) * blk, (zz % 2 + 1) * blk)

    def prepare_coarse():
        @pl.loop(0, pieces)
        def _(c):
            load(1, c).wait()
            for zz in range(part):
                slices(1, c * part + zz, c * (part // 2) + zz // 2, columns(zz))

    def fine_step(t, src, sink, keep=True, turn=0, forcing=forc_ref, span=None):
        def emit(z, s):
            value = s + forcing_at(forcing, t, z)
            if keep:
                put(1 - src, z, value)
            sink(z, value)

        propagate(src, 0, DELTA, emit, turn, span)

    def store_to(buf):
        def emit(z, value):
            buf[z] = value

        return emit

    def drop(z, value):
        pass

    partner = me + 1 - 2 * odd
    swap = pltpu.make_async_remote_copy(
        src_ref=forc_ref, dst_ref=next_ref, send_sem=next_send, recv_sem=next_recv,
        device_id={"tm": partner}, device_id_type=MESH,
    )
    middle = pieces // 2

    def open_up(t, src, start):
        half = part // 2
        for c in range(pieces):
            load(0, c).wait()
            if c == pieces - 1:
                for later in range(pieces):
                    load(1, later).start()
            if c == middle:
                for copy in state_loads:
                    copy.wait()
            for zz in range(part):
                z = c * part + zz
                slices(0, z, z // 2, columns(zz))
            if c == middle:
                for z in range(zones):
                    put(src, z, start(z))
            if c > middle:
                fine_step(t, src, drop, span=range(0 if c == middle + 1 else (c - 1) * half, c * half))
        fine_step(t, src, drop, span=range((pieces - 1) * half if pieces > 2 else 0, pairs))
        pl.semaphore_wait(barrier, n - 1)
        swap.start()

    @pl.when(me == 0)
    def _():
        open_up(0, 0, initial_at)
        fine_step(1, 1, drop, turn=1)
        fine_step(2, 0, drop, turn=2)
        fine_step(3, 1, store_to(ubuf), turn=3)

    @pl.when(me > 0)
    def _():
        open_up(1, 1, functools.partial(forcing_at, forc_ref, 0))
        for t in range(2, M):
            fine_step(t, t % 2, store_to(ubuf) if t == M - 1 else drop, keep=t < M - 1, turn=t - 1)

    onward = pltpu.make_async_remote_copy(
        src_ref=ubuf, dst_ref=carr, send_sem=carr_send, recv_sem=carr_recv,
        device_id={"tm": jnp.where(me == 0, 1, lax.rem(me + 2, n))}, device_id_type=MESH,
    )
    hands_on = jnp.logical_or(me == 0, jnp.logical_and(odd == 1, me < n - 2))

    @pl.when(jnp.logical_and(hands_on, me > 0))
    def _():
        onward.start()

    def interval(sink, beside=None, turn=0):
        for t in range(M):
            fine_step(
                t, t % 2, sink if t == M - 1 else drop, keep=t < M - 1, turn=turn + max(t - 1, 0), forcing=next_ref
            )
            if t == 0 and beside is not None:
                beside()

    def share(target, j):
        return pltpu.make_async_remote_copy(
            src_ref=rbuf.at[j], dst_ref=rbuf.at[j], send_sem=r_send.at[target], recv_sem=r_recv.at[j],
            device_id={"tm": target}, device_id_type=MESH,
        )

    def forward(j):
        return pltpu.make_async_remote_copy(
            src_ref=rbuf.at[j], dst_ref=rbuf.at[j], send_sem=fwd_send.at[j], recv_sem=r_recv.at[j],
            device_id={"tm": lax.rem(me + n - 1, n)}, device_id_type=MESH,
        )

    first_targets = (3, 1)
    far_targets = range(n - 1, 2, -2)

    def each_share(act):
        for target in far_targets:

            @pl.when(jnp.logical_and(me > 1, me < target))
            def _():
                act(share(target, partner))

        @pl.when(jnp.logical_and(odd == 1, me > 1))
        def _():
            act(share(partner, partner))

    @pl.when(me == 0)
    def _():
        swap.wait_recv()
        interval(store_to(rbuf.at[1]), turn=4)
        onward.start()
        for target in first_targets:
            share(target, 1).start()
        for z in range(zones):
            rbuf[0, z] = ubuf[z]

    prepare_coarse()

    @pl.when(jnp.logical_and(odd == 0, me > 0))
    def _():
        for z in range(zones):
            put(0, z, ubuf[z])
        swap.wait_recv()

    @pl.when(odd == 1)
    def _():
        onward.wait_recv()
        for z in range(zones):
            put(0, z, carr[z])
        swap.wait_recv()

    @pl.when(me > 1)
    def _():
        def right_side(z, value):
            rbuf[partner, z] = value - pbuf[z]

        interval(right_side, lambda: propagate(0, 1, coarse_dt, store_to(pbuf)))

    @pl.when(me == 3)
    def _():
        forward(1).wait_recv()
        forward(1).start()
        for z in range(zones):
            put(0, z, rbuf[1, z])

        def second(z, value):
            rbuf[2, z] = value + rbuf[2, z]

        propagate(0, 1, coarse_dt, second)

    each_share(lambda copy: copy.start())

    def arrive(j):
        forward(j).wait_recv()

        @pl.when(jnp.logical_and(odd == 1, j < me - 1))
        def _():
            forward(j).start()

    @pl.when(me == 0)
    def _():
        for z in range(zones):
            put(0, z, initial_at(z))

    @pl.when(me == 1)
    def _():
        for z in range(zones):
            put(0, z, carr[z])

    @pl.when(me == 2)
    def _():
        forward(1).wait_recv()
        for z in range(zones):
            put(0, z, rbuf[1, z])

    @pl.when(me > 3)
    def _():
        arrive(2)

    @pl.when(me > 2)
    def _():
        first = lax.rem(me + 1, 2)
        for z in range(zones):
            put(first, z, rbuf[2, z])

    def reach(left_over):
        j = me - 1 - left_over
        if left_over > 0:
            arrive(j)
        else:

            @pl.when(odd == 0)
            def _():
                arrive(j)

    def chain(left_over, turn=0):
        def emit(z, value):
            put(left_over % 2, z, value + rbuf[me - 1 - left_over, z])

        propagate((left_over + 1) % 2, 1, coarse_dt, emit, turn)

    for left_over in range(n - 5, -1, -1):
        if left_over % 2 == 0:

            @pl.when(me == left_over + 4)
            def _():
                reach(left_over)
                chain(left_over)

        else:

            @pl.when(me > left_over + 3)
            def _():
                reach(left_over)
                reach(left_over - 1)
                chain(left_over)
                chain(left_over - 1, 1)

    @pl.when(me > 0)
    def _():
        forward(me).wait_recv()

    def corner(z, value):
        emit_out(M - 1, z, jnp.where(me > 2, value, 0.0) + rbuf[me, z])

    for t in range(M - 1):
        fine_step(t, t % 2, functools.partial(emit_out, t), keep=t < M - 2, turn=max(t - 1, 0))
        if t == 0:
            propagate(0, 1, coarse_dt, corner)

    swap.wait_send()

    @pl.when(hands_on)
    def _():
        onward.wait_send()

    @pl.when(me == 0)
    def _():
        for target in first_targets:
            share(target, 1).wait_send()

    each_share(lambda copy: copy.wait_send())

    def drain(j, _):
        forward(j).wait_send()
        return 0

    lax.fori_loop(jnp.where(me == 3, 1, 2), jnp.where(odd == 1, me - 1, 2), drain, 0)


def solution(mesh):
    n = mesh.shape["tm"]

    def body(initial, forcing, fine_blocks, coarse_blocks):
        inst, slots, cells = forcing.shape
        zones, _, blk, _ = fine_blocks.shape
        blocks = cells // blk
        reps = blocks // zones
        rows = inst * reps
        assert slots == M and n > 4 and n % 2 == 0 and zones % 2 == 0
        pieces = 4 if zones % 4 == 0 else 1
        init_rows = initial.reshape(inst, blocks, blk).transpose(1, 0, 2).reshape(-1, blk)
        forc_rows = forcing.reshape(inst, slots, blocks, blk).transpose(0, 2, 1, 3).reshape(-1, blk)
        state = pltpu.VMEM((zones, rows, blk), jnp.float32)
        out = pl.pallas_call(
            functools.partial(kernel, n, inst, zones, reps, pieces),
            out_shape=pltpu.VMEM(forc_rows.shape, jnp.float32),
            in_specs=[pl.BlockSpec(memory_space=pltpu.HBM)] * 4,
            out_specs=pl.BlockSpec(memory_space=pltpu.VMEM),
            scratch_shapes=[
                pltpu.VMEM(init_rows.shape, jnp.float32),
                pltpu.VMEM(forc_rows.shape, jnp.float32),
                pltpu.VMEM(forc_rows.shape, jnp.float32),
                pltpu.VMEM((2,) + fine_blocks.shape, jnp.float32),
                pltpu.VMEM((2, zones, 3 * blk, 2 * blk), F8),
                pltpu.VMEM((2, zones // 2, 3 * blk, 2 * blk), F8),
                pltpu.VMEM((2, zones + 2, 2 * rows, blk), jnp.bfloat16),
                state,
                state,
                pltpu.VMEM((n, zones, rows, blk), jnp.float32),
                state,
                pltpu.SemaphoreType.DMA((2, pieces)),
                pltpu.SemaphoreType.DMA((2,)),
                pltpu.SemaphoreType.DMA,
                pltpu.SemaphoreType.DMA,
                pltpu.SemaphoreType.DMA,
                pltpu.SemaphoreType.DMA,
                pltpu.SemaphoreType.DMA((n,)),
                pltpu.SemaphoreType.DMA((n,)),
                pltpu.SemaphoreType.DMA((n,)),
            ],
            compiler_params=pltpu.CompilerParams(collective_id=0, has_side_effects=True),
        )(init_rows, forc_rows, fine_blocks, coarse_blocks)
        return out.reshape(inst, blocks, slots, blk).transpose(0, 2, 1, 3).reshape(forcing.shape)

    in_specs = (P("grp", None), P("grp", "tm", None), P(), P())
    out_specs = P("grp", "tm", None)
    return jax.shard_map(body, mesh=mesh, in_specs=in_specs, out_specs=out_specs, check_vma=False)
```

time: 18.8 us -> 18.1 us (0.963)
  Pallas kernels: 17.8 us -> 17.1 us
    pallas_call x1, Pallas kernels: 17.8 us -> 17.1 us  [body(): pl.pallas_call(functools.partial(kernel, n, inst, zones, reps, pieces), o...]
where the time goes in v2:
time: 18.1 us; the launch traced here: 17.9 us
  Pallas kernels  17.1 us (94%)
  local copies, waits for them, and re-layouts  0.8 us (4%)
    pallas_call x1, Pallas kernels, body(): pl.pallas_call(functools.partial(kernel, n, inst, zones, reps, pieces), o...  17.1 us
    unnamed x1, local copies, waits for them, and re-layouts  0.8 us

profile of v2, /device:TPU:30, one launch (start us, length us, event | category | flops | bytes accessed | tf_op | source)
XLA Modules:
  0.0 17.9 jit_solution(10621912745175092254)
XLA Ops:
  0.0 17.1 %shard_map.46 = f32[1024,128]{1,0:T(8,128)S(1)} custom-call(f32[256,128]{1,0:T(8,128)} %bitcast.17, f32[1024,128]{1,0:T(8,128)} %bitcast.16, f32[16,3,128,128]{3,2,1,0:T(8,128)} %fine_hbm.1, f32[16,3,128,128]{3,2,1,0:T(8,128)} %coarse_hbm.1), custom_call_target="tpu_custom_call" | custom-call | tf_op jit(solution)/shard_map/pallas_call | solution.py:400
  17.1 0.8 %copy.9 = f32[2,4,16384]{2,1,0:T(4,128)} copy(f32[2,4,16384]{2,1,0:T(4,128)S(1)} %bitcast.15) | data formatting | bytes 1048576

commit v3 on v2

v3 whole, which is shorter than its diff:
```python
import functools

import jax
import jax.numpy as jnp
from jax import lax
from jax.experimental import pallas as pl
from jax.experimental.pallas import tpu as pltpu
from jax.sharding import PartitionSpec as P

M = 4
DELTA = 0.05
MESH = pl.DeviceIdType.MESH
F8 = jnp.float8_e4m3fn


def newton(mixing, delta_t):
    solved = mixing
    for _ in range(2):
        squared = solved * solved
        solved = (mixing + (2.0 * delta_t) * solved * squared) / (
            (1.0 - delta_t) + (3.0 * delta_t) * squared
        )
    return solved


LIFTS = (2.0**8, 1.0, 2.0**10)
HALVES = 2


def kernel(
    n, inst, zones, reps, pieces,
    init_hbm, forc_hbm, fine_hbm, coarse_hbm, out_ref,
    init_ref, forc_ref, next_ref, raw, upper, lower, x, start_x, ubuf, carr, rbuf, pbuf,
    load_sem, state_sem, next_send, next_recv, carr_send, carr_recv, r_send, r_recv, fwd_send,
):
    me = lax.axis_index("tm")
    blk = raw.shape[-1]
    rows = inst * reps
    coarse_dt = DELTA * M
    part = zones // pieces
    pairs = zones // 2
    odd = lax.rem(me, 2)

    eighth = zones // 8
    fine_cuts = [e * eighth for e in (0, 1, 3, 5, 7, 8)] if eighth > 1 and eighth % 2 == 0 else [0, zones]
    blocks = len(fine_cuts) - 1

    def load(c):
        span = pl.ds(fine_cuts[c], fine_cuts[c + 1] - fine_cuts[c])
        return pltpu.make_async_copy(fine_hbm.at[span], raw.at[0, span], load_sem.at[c])

    coarse_load = pltpu.make_async_copy(coarse_hbm, raw.at[1], load_sem.at[blocks])

    state_loads = [
        pltpu.make_async_copy(init_hbm, init_ref, state_sem.at[0]),
        pltpu.make_async_copy(forc_hbm, forc_ref, state_sem.at[1]),
    ]
    state_loads[0].start()
    load(0).start()
    state_loads[1].start()
    for c in range(1, blocks):
        load(c).start()

    barrier = pltpu.get_barrier_semaphore()
    for step in range(1, n):
        pl.semaphore_signal(barrier, inc=1, device_id={"tm": lax.rem(me + step, n)}, device_id_type=MESH)

    def initial_at(z):
        return jnp.concatenate(
            [init_ref[pl.ds(z * inst + i, reps, stride=zones * inst), :] for i in range(inst)], axis=0
        )

    def forcing_at(ref, slot, z):
        return jnp.concatenate(
            [ref[pl.ds((i * reps * zones + z) * M + slot, reps, stride=zones * M), :] for i in range(inst)],
            axis=0,
        )

    def emit_out(slot, z, value):
        for i in range(inst):
            out_ref[pl.ds((i * reps * zones + z) * M + slot, reps, stride=zones * M), :] = value[
                i * reps : (i + 1) * reps
            ]

    row = lax.broadcasted_iota(jnp.int32, (rows, blk), 0)

    def state_of(where):
        return x.at[where] if isinstance(where, int) else where

    def put(dst, z, value):
        held = state_of(dst)

        def write(slot, v):
            high = v.astype(jnp.bfloat16)
            low = (v - high.astype(jnp.float32)).astype(jnp.bfloat16)
            held[slot, :rows] = high
            held[slot, rows:] = low

        write(z + 1, value)
        if z == 0:
            rolled = pltpu.roll(value, rows - 1, 0)
            write(zones + 1, jnp.where(row % reps == reps - 1, 0.0, rolled))
        if z == zones - 1:
            rolled = pltpu.roll(value, 1, 0)
            write(0, jnp.where(row % reps == 0, 0.0, rolled))

    def propagate(src, which, delta_t, emit, turn=0, span=None):
        held = state_of(src)
        for q in range(pairs) if span is None else span:
            p = (q + turn) % pairs
            z = 2 * p

            def left(i, stop):
                return jnp.concatenate([held[z + i + k, :stop] for k in range(3)], axis=1)

            tail = jnp.dot(
                jnp.concatenate([left(0, rows), left(1, rows)], axis=0),
                lower[which, p], preferred_element_type=jnp.float32,
            )
            for i in range(2):
                acc = jnp.dot(left(i, 2 * rows), upper[which, z + i], preferred_element_type=jnp.float32)
                cols = slice(i * blk, (i + 1) * blk)
                second = acc[:rows, blk:] + acc[rows:, blk:] + tail[i * rows : (i + 1) * rows, cols] * (1.0 / LIFTS[2])
                total = acc[:rows, :blk] + acc[rows:, :blk] + second
                emit(z + i, newton(total * (1.0 / LIFTS[0]), delta_t))

    def slices(which, z, p, cols):
        for k in range(3):
            span = slice(k * blk, (k + 1) * blk)
            rest = raw[which, z, k].T
            for s, lift in enumerate(LIFTS):
                if lift != 1.0:
                    rest = rest * lift
                piece = rest.astype(F8)
                if s < 2:
                    upper[which, z, span, s * blk : (s + 1) * blk] = piece
                    rest = rest - piece.astype(jnp.float32)
                else:
                    lower[which, p, span, cols] = piece

    def columns(zz):
        return slice((zz % 2) * blk, (zz % 2 + 1) * blk)

    def prepare_coarse():
        coarse_load.wait()

        @pl.loop(0, pieces)
        def _(c):
            for zz in range(part):
                slices(1, c * part + zz, c * (part // 2) + zz // 2, columns(zz))

    def fine_step(t, src, sink, keep=True, turn=0, forcing=forc_ref, span=None):
        def emit(z, s):
            value = s + forcing_at(forcing, t, z)
            if keep:
                put(1 - src, z, value)
            sink(z, value)

        propagate(src, 0, DELTA, emit, turn, span)

    def store_to(buf):
        def emit(z, value):
            buf[z] = value

        return emit

    def drop(z, value):
        pass

    partner = me + 1 - 2 * odd
    half = zones // HALVES
    parts_of = [range(h * (pairs // HALVES), (h + 1) * (pairs // HALVES)) for h in range(HALVES)]
    swap = pltpu.make_async_remote_copy(
        src_ref=forc_ref, dst_ref=next_ref, send_sem=next_send, recv_sem=next_recv,
        device_id={"tm": partner}, device_id_type=MESH,
    )

    def open_up(t, src, start):
        state_at = max(blocks - 2, 0)
        done = 0
        for c in range(blocks):
            load(c).wait()
            if c == state_at:
                coarse_load.start()
                for copy in state_loads:
                    copy.wait()
                for z in range(zones):
                    put(src, z, start(z))
            if c >= state_at:
                fine_step(t, src, drop, span=range(done, fine_cuts[c] // 2))
                done = fine_cuts[c] // 2
            for z in range(fine_cuts[c], fine_cuts[c + 1]):
                slices(0, z, z // 2, columns(z))
        fine_step(t, src, drop, span=range(done, pairs))
        pl.semaphore_wait(barrier, n - 1)
        swap.start()

    @pl.when(me == 0)
    def _():
        open_up(0, 0, initial_at)
        fine_step(1, 1, drop, turn=1)
        fine_step(2, 0, drop, turn=2)
        fine_step(3, 1, store_to(ubuf), turn=3)

    def onward(h):
        span = pl.ds(h * half, half)
        return pltpu.make_async_remote_copy(
            src_ref=ubuf.at[span], dst_ref=carr.at[span], send_sem=carr_send.at[h], recv_sem=carr_recv.at[h],
            device_id={"tm": jnp.where(me == 0, 1, lax.rem(me + 2, n))}, device_id_type=MESH,
        )

    hands_on = jnp.logical_and(odd == 1, me < n - 2)

    @pl.when(me > 0)
    def _():
        open_up(1, 1, functools.partial(forcing_at, forc_ref, 0))
        for t in range(2, M - 1):
            fine_step(t, t % 2, drop, turn=t + 1)
        for h in (1, 0):
            fine_step(M - 1, (M - 1) % 2, store_to(ubuf), keep=False, turn=pairs // 2, span=parts_of[1 - h])

            @pl.when(hands_on)
            def _():
                onward(h).start()

    def interval(sink, beside=None, turn=0, mid=None):
        for t in range(M):
            args = dict(keep=t < M - 1, turn=turn + t + (beside is not None and t > 0), forcing=next_ref)
            if t < M - 1:
                fine_step(t, t % 2, drop, **args)
            else:
                for h in range(HALVES):
                    fine_step(t, t % 2, sink, span=parts_of[h], **args)
                    if mid is not None:
                        mid(h)
            if t == 0 and beside is not None:
                beside()

    def message(j, h):
        return rbuf.at[j, pl.ds(h * half, half)] if h is not None else rbuf.at[j]

    def landed(j, h):
        return r_recv.at[j if not h else n + j - 1]

    def share(target, j, h):
        return pltpu.make_async_remote_copy(
            src_ref=message(j, h), dst_ref=message(j, h), send_sem=r_send.at[target // 2, h or 0],
            recv_sem=landed(j, h), device_id={"tm": target}, device_id_type=MESH,
        )

    def forward(j, h):
        return pltpu.make_async_remote_copy(
            src_ref=message(j, h), dst_ref=message(j, h), send_sem=fwd_send.at[j if not h else 0],
            recv_sem=landed(j, h), device_id={"tm": lax.rem(me + n - 1, n)}, device_id_type=MESH,
        )

    first_targets = (3, 1)
    far_targets = range(3, n, 2)

    def each_share(act, h):
        for target in far_targets:

            @pl.when(jnp.logical_and(me > 1, me < target))
            def _():
                act(share(target, partner, h))

        @pl.when(jnp.logical_and(odd == 1, me > 1))
        def _():
            act(share(partner, partner, h))

    def start(copy):
        copy.start()

    def wait_send(copy):
        copy.wait_send()

    @pl.when(me == 0)
    def _():
        swap.wait_recv()

        def first_share(h):
            for target in first_targets:
                share(target, 1, h).start()

        interval(store_to(rbuf.at[1]), turn=M + 1, mid=first_share)
        for h in range(HALVES):
            onward(h).start()
        for z in range(zones):
            rbuf[0, z] = ubuf[z]

    prepare_coarse()

    @pl.when(jnp.logical_and(odd == 0, me > 0))
    def _():
        for z in range(zones):
            put(0, z, ubuf[z])
        swap.wait_recv()

    @pl.when(odd == 1)
    def _():
        for h in (1, 0):
            onward(h).wait_recv()
            for z in range(h * half, (h + 1) * half):
                put(0, z, carr[z])
        swap.wait_recv()

    @pl.when(me > 1)
    def _():
        def right_side(z, value):
            rbuf[partner, z] = value - pbuf[z]

        interval(right_side, lambda: propagate(0, 1, coarse_dt, store_to(pbuf)))

    early = list(range(1, parts_of[0].stop - 1))
    late = [p for p in range(pairs) if p not in early]
    late = [[p for p in late if p in parts_of[0]], [p for p in late if p not in parts_of[0]]]

    @pl.when(me == 3)
    def _():
        def second(z, value):
            rbuf[2, z] = value + rbuf[2, z]

        for h in range(HALVES):
            forward(1, h).wait_recv()
            for z in range(h * half, (h + 1) * half):
                put(0, z, rbuf[1, z])
            if h == 0:
                propagate(0, 1, coarse_dt, second, span=early)
        forward(1, None).start()
        for h in range(HALVES):
            propagate(0, 1, coarse_dt, second, span=late[h])
            each_share(start, h)

    @pl.when(me != 3)
    def _():
        each_share(start, None)

    def arrive(j, h=None):
        forward(j, h).wait_recv()

        @pl.when(jnp.logical_and(odd == 1, j < me - 1))
        def _():
            forward(j, h).start()

    @pl.when(me == 0)
    def _():
        for z in range(zones):
            put(0, z, initial_at(z))

    @pl.when(me == 1)
    def _():
        for z in range(zones):
            put(0, z, carr[z])

    @pl.when(me == 2)
    def _():
        forward(1, None).wait_recv()
        for z in range(zones):
            put(0, z, rbuf[1, z])

    for j in range(3, n - 1, 2):

        @pl.when(me > j)
        def _():
            arrive(j)

    @pl.when(me == 3)
    def _():
        for z in range(zones):
            put(0, z, rbuf[2, z])

    def chain(src, dst, j, span=None, turn=0):
        def emit(z, value):
            put(dst, z, value + rbuf[j, z])

        propagate(src, 1, coarse_dt, emit, turn, span)

    def begin(parity):
        for h in range(HALVES):
            arrive(2, h)
            for z in range(h * half, (h + 1) * half):
                put(start_x, z, rbuf[2, z])
            if h == 0:
                chain(start_x, parity, 3, early)
        if parity == 1:

            @pl.when(me > 5)
            def _():
                arrive(4)

        chain(start_x, parity, 3, late[0][1:] + late[1] + late[0][:1])
        if parity == 1:
            chain(1, 0, 4, turn=late[0][-1] + 1)

    for parity in range(2):

        @pl.when(jnp.logical_and(me > 3, odd == parity))
        def _():
            begin(parity)

    for left_over in range(n - 5 - n % 2, 0, -1):
        if left_over % 2 == 1:

            @pl.when(me > left_over + 4)
            def _():
                j = me - 1 - left_over

                @pl.when(jnp.logical_or(odd == 0, left_over > 1))
                def _():
                    arrive(j + odd)

                chain(0, 1, j)
                chain(1, 0, j + 1, turn=1)

    @pl.when(jnp.logical_or(me == 1, me == 2))
    def _():
        for h in range(HALVES):
            forward(me, h).wait_recv()

    @pl.when(me > 2)
    def _():
        forward(me, None).wait_recv()

    def corner(z, value):
        emit_out(M - 1, z, jnp.where(me > 2, value, 0.0) + rbuf[me, z])

    for t in range(M - 1):
        fine_step(t, t % 2, functools.partial(emit_out, t), keep=t < M - 2, turn=max(t - 1, 0))
        if t == 0:
            propagate(0, 1, coarse_dt, corner)

    swap.wait_send()
    for h in range(HALVES):

        @pl.when(jnp.logical_or(hands_on, me == 0))
        def _():
            onward(h).wait_send()

        @pl.when(me == 0)
        def _():
            for target in first_targets:
                share(target, 1, h).wait_send()

        @pl.when(me == 3)
        def _():
            each_share(wait_send, h)

    @pl.when(me != 3)
    def _():
        each_share(wait_send, None)

    @pl.when(me == 3)
    def _():
        forward(1, None).wait_send()

    @pl.when(jnp.logical_and(odd == 1, me > 3))
    def _():
        for h in range(HALVES):
            forward(2, h).wait_send()

    def drain(j, _):
        forward(j, None).wait_send()
        return 0

    lax.fori_loop(3, jnp.where(odd == 1, me - 1, 3), drain, 0)


def solution(mesh):
    n = mesh.shape["tm"]

    def body(initial, forcing, fine_blocks, coarse_blocks):
        inst, slots, cells = forcing.shape
        zones, _, blk, _ = fine_blocks.shape
        blocks = cells // blk
        reps = blocks // zones
        rows = inst * reps
        assert slots == M and n > 4 and n % 2 == 0 and zones % (2 * HALVES) == 0
        pieces = 4 if zones % 4 == 0 else 1
        init_rows = initial.reshape(inst, blocks, blk).transpose(1, 0, 2).reshape(-1, blk)
        forc_rows = forcing.reshape(inst, slots, blocks, blk).transpose(0, 2, 1, 3).reshape(-1, blk)
        state = pltpu.VMEM((zones, rows, blk), jnp.float32)
        out = pl.pallas_call(
            functools.partial(kernel, n, inst, zones, reps, pieces),
            out_shape=pltpu.VMEM(forc_rows.shape, jnp.float32),
            in_specs=[pl.BlockSpec(memory_space=pltpu.HBM)] * 4,
            out_specs=pl.BlockSpec(memory_space=pltpu.VMEM),
            scratch_shapes=[
                pltpu.VMEM(init_rows.shape, jnp.float32),
                pltpu.VMEM(forc_rows.shape, jnp.float32),
                pltpu.VMEM(forc_rows.shape, jnp.float32),
                pltpu.VMEM((2,) + fine_blocks.shape, jnp.float32),
                pltpu.VMEM((2, zones, 3 * blk, 2 * blk), F8),
                pltpu.VMEM((2, zones // 2, 3 * blk, 2 * blk), F8),
                pltpu.VMEM((2, zones + 2, 2 * rows, blk), jnp.bfloat16),
                pltpu.VMEM((zones + 2, 2 * rows, blk), jnp.bfloat16),
                state,
                state,
                pltpu.VMEM((n, zones, rows, blk), jnp.float32),
                state,
                pltpu.SemaphoreType.DMA((6,)),
                pltpu.SemaphoreType.DMA((2,)),
                pltpu.SemaphoreType.DMA,
                pltpu.SemaphoreType.DMA,
                pltpu.SemaphoreType.DMA((HALVES,)),
                pltpu.SemaphoreType.DMA((HALVES,)),
                pltpu.SemaphoreType.DMA((n // 2, HALVES)),
                pltpu.SemaphoreType.DMA((n + 2,)),
                pltpu.SemaphoreType.DMA((n - 2,)),
            ],
            compiler_params=pltpu.CompilerParams(collective_id=0, has_side_effects=True),
        )(init_rows, forc_rows, fine_blocks, coarse_blocks)
        return out.reshape(inst, blocks, slots, blk).transpose(0, 2, 1, 3).reshape(forcing.shape)

    in_specs = (P("grp", None), P("grp", "tm", None), P(), P())
    out_specs = P("grp", "tm", None)
    return jax.shard_map(body, mesh=mesh, in_specs=in_specs, out_specs=out_specs, check_vma=False)
```

time: 18.1 us -> 17 us (0.939)
  Pallas kernels: 17.1 us -> 16.1 us
    pallas_call x1, Pallas kernels: 17.1 us -> 16.1 us  [body(): pl.pallas_call(functools.partial(kernel, n, inst, zones, reps, pieces), o...]
where the time goes in v3:
time: 17 us; the launch traced here: 16.9 us
  Pallas kernels  16.1 us (95%)
  local copies, waits for them, and re-layouts  0.8 us (5%)
    pallas_call x1, Pallas kernels, body(): pl.pallas_call(functools.partial(kernel, n, inst, zones, reps, pieces), o...  16.1 us
    unnamed x1, local copies, waits for them, and re-layouts  0.8 us

profile of v3, /device:TPU:30, one launch (start us, length us, event | category | flops | bytes accessed | tf_op | source)
XLA Modules:
  0.0 16.9 jit_solution(15746366018440338844)
XLA Ops:
  0.0 16.1 %shard_map.46 = f32[1024,128]{1,0:T(8,128)S(1)} custom-call(f32[256,128]{1,0:T(8,128)} %bitcast.17, f32[1024,128]{1,0:T(8,128)} %bitcast.16, f32[16,3,128,128]{3,2,1,0:T(8,128)} %fine_hbm.1, f32[16,3,128,128]{3,2,1,0:T(8,128)} %coarse_hbm.1), custom_call_target="tpu_custom_call" | custom-call | tf_op jit(solution)/shard_map/pallas_call | solution.py:482
  16.1 0.8 %copy.9 = f32[2,4,16384]{2,1,0:T(4,128)} copy(f32[2,4,16384]{2,1,0:T(4,128)S(1)} %bitcast.15) | data formatting | bytes 1048576

commit v4 on v3

--- a/solution.py
+++ b/solution.py
@@ -369,34 +369,60 @@
         for z in range(zones):
             put(0, z, rbuf[2, z])
 
+    @pl.when(jnp.logical_or(me == 1, me == 2))
+    def _():
+        for h in range(HALVES):
+            forward(me, h).wait_recv()
+
+    @pl.when(me > 2)
+    def _():
+        forward(me, None).wait_recv()
+
+    def corner(z, value):
+        emit_out(M - 1, z, jnp.where(me > 2, value, 0.0) + rbuf[me, z])
+
+    def finish(turn=0):
+        for t in range(M - 1):
+            fine_step(t, t % 2, functools.partial(emit_out, t), keep=t < M - 2, turn=turn + t + (t > 0))
+            if t == 0:
+                propagate(0, 1, coarse_dt, corner, turn)
+
     def chain(src, dst, j, span=None, turn=0):
         def emit(z, value):
             put(dst, z, value + rbuf[j, z])
 
         propagate(src, 1, coarse_dt, emit, turn, span)
 
-    def begin(parity):
+    def begin(parity, last):
         for h in range(HALVES):
             arrive(2, h)
             for z in range(h * half, (h + 1) * half):
                 put(start_x, z, rbuf[2, z])
             if h == 0:
                 chain(start_x, parity, 3, early)
+        if parity == 1 and not last:
+            arrive(4)
+        chain(start_x, parity, 3, late[0][1:] + late[1] + late[0][:1])
+        turn = late[0][-1] + 1
         if parity == 1:
-
-            @pl.when(me > 5)
-            def _():
-                arrive(4)
-
-        chain(start_x, parity, 3, late[0][1:] + late[1] + late[0][:1])
-        if parity == 1:
-            chain(1, 0, 4, turn=late[0][-1] + 1)
+            chain(1, 0, 4, turn=turn)
+            turn += 1
+        if last:
+            finish(turn)
+
+    @pl.when(me < 4)
+    def _():
+        finish()
 
     for parity in range(2):
 
-        @pl.when(jnp.logical_and(me > 3, odd == parity))
-        def _():
-            begin(parity)
+        @pl.when(me == 4 + parity)
+        def _():
+            begin(parity, True)
+
+        @pl.when(jnp.logical_and(me > 5, odd == parity))
+        def _():
+            begin(parity, False)
 
     for left_over in range(n - 5 - n % 2, 0, -1):
         if left_over % 2 == 1:
@@ -411,23 +437,8 @@
 
                 chain(0, 1, j)
                 chain(1, 0, j + 1, turn=1)
-
-    @pl.when(jnp.logical_or(me == 1, me == 2))
-    def _():
-        for h in range(HALVES):
-            forward(me, h).wait_recv()
-
-    @pl.when(me > 2)
-    def _():
-        forward(me, None).wait_recv()
-
-    def corner(z, value):
-        emit_out(M - 1, z, jnp.where(me > 2, value, 0.0) + rbuf[me, z])
-
-    for t in range(M - 1):
-        fine_step(t, t % 2, functools.partial(emit_out, t), keep=t < M - 2, turn=max(t - 1, 0))
-        if t == 0:
-            propagate(0, 1, coarse_dt, corner)
+                if left_over == 1:
+                    finish(2)
 
     swap.wait_send()
     for h in range(HALVES):

time: 17 us -> 16.9 us (level)
  Pallas kernels: 16.1 us -> 15.9 us
where the time goes in v4:
time: 16.9 us; the launch traced here: 16.7 us
  Pallas kernels  15.9 us (94%)
  local copies, waits for them, and re-layouts  0.8 us (5%)
    pallas_call x1, Pallas kernels, body(): pl.pallas_call(functools.partial(kernel, n, inst, zones, reps, pieces), o...  15.9 us
    unnamed x1, local copies, waits for them, and re-layouts  0.8 us

profile of v4, /device:TPU:30, one launch (start us, length us, event | category | flops | bytes accessed | tf_op | source)
XLA Modules:
  0.0 16.7 jit_solution(8133283558913553108)
XLA Ops:
  0.0 15.9 %shard_map.46 = f32[1024,128]{1,0:T(8,128)S(1)} custom-call(f32[256,128]{1,0:T(8,128)} %bitcast.17, f32[1024,128]{1,0:T(8,128)} %bitcast.16, f32[16,3,128,128]{3,2,1,0:T(8,128)} %fine_hbm.1, f32[16,3,128,128]{3,2,1,0:T(8,128)} %coarse_hbm.1), custom_call_target="tpu_custom_call" | custom-call | tf_op jit(solution)/shard_map/pallas_call | solution.py:493
  15.9 0.8 %copy.9 = f32[2,4,16384]{2,1,0:T(4,128)} copy(f32[2,4,16384]{2,1,0:T(4,128)S(1)} %bitcast.15) | data formatting | bytes 1048576
